TPU v7x, 256 devices: a 2x2x32 block of a 4x8x32 slice. The times are simulated.
256 devices in a mesh: groups: 4 (over x, y), seq: 32 (over z), head: 2 (over core).
Axes of the slice: x: 2, y: 2, z: 32, core: 2. Of those that a mesh axis runs over, the one named last changes fastest.
The devices are a block of a 4x8x32 slice.
Arguments:
- queries: bfloat16 [16384, 28, 128], P(('groups', 'seq'), 'head'), parts along dimension 0, may hold values from -400 to 400, as said below
- request_image: int32 [16384, 1], P(('groups', 'seq')), parts along dimension 0, may hold values from 0 to 63; in each aligned block of 128 rows (0 to 127, 128 to 255, ...) at most 4 rows name the same one
- image_slot: int32 [256], P('groups'), parts along dimension 0, may hold values from 0 to 63, each once
- image_lengths: int32 [256], P(('groups', 'seq')), parts along dimension 0, may hold values from 640 to 1280
- image_keys: bfloat16 [256, 4, 1280, 128], P(('groups', 'seq'), 'head'), parts along dimension 0, may hold values from -6 to 6
- image_values: bfloat16 [256, 4, 1280, 128], P(('groups', 'seq'), 'head'), parts along dimension 0, may hold values from -6 to 6
- text_keys: bfloat16 [16384, 4, 64, 128], P(('groups', 'seq'), 'head'), parts along dimension 0, may hold values from -6 to 6
- text_values: bfloat16 [16384, 4, 64, 128], P(('groups', 'seq'), 'head'), parts along dimension 0, may hold values from -6 to 6
- text_lengths: int32 [16384], P(('groups', 'seq')), parts along dimension 0, may hold values from 1 to 64
Outputs:
- attention: bfloat16 [16384, 28, 128], P(('groups', 'seq'), 'head'), parts along dimension 0
There are 4 independent parts, one for each index of `groups`. A program takes and returns all parts, laid end to end along the dimension named above; each array names one. Nothing has to cross between parts.
Inputs may be any that keep to these rules, and one draw needn't show every extreme that they name: queries are finite bfloat16 values. `request_image`: the requests of one index of seq name any one image at most 4 times, and in some index of seq some image is named exactly 4 times. `image_slot`: a permutation; the image in storage slot s is held by index s // 2 of seq.
All inputs are finite; a program needn't handle non-finite values.
Results may differ from a plain program's by a relative error of at most 0.0056.
Values may be sent and summed in bfloat16 or wider, within the bound.
A program may use at most 64 MiB of HBM per device.

v0:
```python
import math

import jax
import jax.numpy as jnp
from jax import lax
from jax.sharding import PartitionSpec as P

NEGATIVE = -1e30


def weigh(scores, valid):
    scores = jnp.where(valid, scores, NEGATIVE)
    highest = jnp.max(scores, axis=-1, keepdims=True)
    weights = jnp.where(valid, jnp.exp(scores - highest), 0.0)
    total = jnp.sum(weights, axis=-1, keepdims=True)
    return (weights.astype(jnp.bfloat16), total, highest)


def on_device(
    queries,
    request_image,
    image_slot,
    image_lengths,
    image_keys,
    image_values,
    text_keys,
    text_values,
    text_lengths,
):
    rows, local_heads, head_size = queries.shape
    local_kv = image_keys.shape[1]
    group = local_heads // local_kv
    images = image_slot.shape[0]
    held = image_keys.shape[0]
    image_tokens = image_keys.shape[2]
    text_tokens = text_keys.shape[2]
    devices = lax.axis_size("seq")
    most = max(2, 2 * rows // images)
    width = local_heads * head_size
    scale = 1.0 / math.sqrt(head_size)
    image_ids = jnp.arange(images, dtype=jnp.int32)
    chosen = request_image == image_ids[None, :]
    slots = jnp.sum(jnp.where(chosen, image_slot[None, :], 0), axis=1)
    slot_hits = (slots[:, None] == image_ids[None, :]).astype(jnp.int32)
    ranks = jnp.sum(slot_hits * (jnp.cumsum(slot_hits, axis=0) - 1), axis=1)
    targets = slots * most + ranks
    dispatch = (jnp.arange(images * most, dtype=jnp.int32)[:, None] == targets[None, :]).astype(
        jnp.bfloat16
    )
    flat_queries = queries.reshape(rows, width)
    outgoing = jnp.dot(dispatch, flat_queries, preferred_element_type=jnp.float32).astype(
        jnp.bfloat16
    )
    outgoing = outgoing.reshape(devices, held, most, width)
    incoming = lax.all_to_all(outgoing, "seq", split_axis=0, concat_axis=0, tiled=True)
    sources = incoming.shape[0]
    count = incoming.shape[2]
    outputs = []
    sums = []
    for index in range(held):
        heads = incoming[:, index].reshape(sources * count, local_kv, group, head_size)
        scores = (
            jnp.einsum(
                "rhgd,htd->rhgt", heads, image_keys[index], preferred_element_type=jnp.float32
            )
            * scale
        )
        valid = jnp.arange(image_tokens, dtype=jnp.int32) < image_lengths[index]
        weights, total, highest = weigh(scores, valid)
        output = (
            jnp.einsum(
                "rhgt,htd->rhgd", weights, image_values[index], preferred_element_type=jnp.float32
            )
            / total
        )
        lse_value = highest[..., 0] + jnp.log(total[..., 0])
        outputs.append(output.astype(jnp.bfloat16).reshape(sources, count, width))
        sums.append(lse_value.reshape(sources, count, local_heads))
    stacked_out = jnp.stack(outputs, axis=1)
    stacked_lse = jnp.stack(sums, axis=1)
    wide_back, back_lse = (
        lax.all_to_all(
            stacked_out.astype(jnp.float32), "seq", split_axis=0, concat_axis=0, tiled=True
        ),
        lax.all_to_all(stacked_lse, "seq", split_axis=0, concat_axis=0, tiled=True),
    )
    back_out = wide_back.astype(jnp.bfloat16)
    flat_back = back_out.reshape(images * most, width)
    image_part = jnp.einsum("sr,sc->rc", dispatch, flat_back, preferred_element_type=jnp.float32)
    image_part = image_part.reshape(rows, local_kv, group, head_size)
    image_lse = jnp.einsum(
        "sr,sc->rc",
        dispatch.astype(jnp.float32),
        back_lse.reshape(images * most, local_heads),
        precision=lax.Precision.HIGHEST,
    )
    image_lse = image_lse.reshape(rows, local_kv, group)
    heads = queries.reshape(rows, local_kv, group, head_size)
    scores = (
        jnp.einsum("rhgd,rhtd->rhgt", heads, text_keys, preferred_element_type=jnp.float32) * scale
    )
    valid = (jnp.arange(text_tokens, dtype=jnp.int32)[None, :] < text_lengths[:, None])[
        :, None, None, :
    ]
    weights, total, highest = weigh(scores, valid)
    text_out = (
        jnp.einsum("rhgt,rhtd->rhgd", weights, text_values, preferred_element_type=jnp.float32)
        / total
    )
    text_lse = highest[..., 0] + jnp.log(total[..., 0])
    upper = jnp.maximum(image_lse, text_lse)
    image_weight = jnp.exp(image_lse - upper)[..., None]
    text_weight = jnp.exp(text_lse - upper)[..., None]
    merged = (image_weight * image_part + text_weight * text_out) / (image_weight + text_weight)
    return merged.reshape(rows, local_heads, head_size).astype(jnp.bfloat16)


def solution(mesh):
    in_specs = (
        P(("groups", "seq"), "head", None),
        P(("groups", "seq"), None),
        P("groups"),
        P(("groups", "seq")),
        P(("groups", "seq"), "head", None, None),
        P(("groups", "seq"), "head", None, None),
        P(("groups", "seq"), "head", None, None),
        P(("groups", "seq"), "head", None, None),
        P(("groups", "seq")),
    )
    out_specs = P(("groups", "seq"), "head", None)
    return jax.shard_map(
        on_device, mesh=mesh, in_specs=in_specs, out_specs=out_specs, check_vma=False
    )
```

profile of v0, /device:TPU:37, one launch (start us, length us, event | category | flops | bytes accessed | tf_op | source)
XLA Modules:
  0.0 288.1 jit_solution(14213206546777209920)
XLA Ops:
  0.0 1.4 copy.69
  1.4 0.8 select_reduce_fusion.1
  2.7 0.5 convolution_convert_fusion
  3.2 1.1 reshape.101
  4.4 33.2 %all-to-all-start = ((bf16[32,2,4,1792]{3,2,1,0:T(4,128)(2,1)}), bf16[32,2,4,1792]{3,2,1,0:T(4,128)(2,1)S(1)}, u32[]{:S(2)}, u32[]{:S(2)}) async-start(bf16[32,2,4,1792]{3,2,1,0:T(4,128)(2,1)} %reshape.101), calls=%async_computation | async-start | bytes 1835008 | tf_op jit(solution)/shard_map/all_to_all | solution.py:55
  37.6 1.3 fusion.83
  38.9 0.6 iota_compare_fusion.4
  39.5 0.7 iota_compare_fusion.5
  40.2 92.5 %all-to-all-done = bf16[32,2,4,1792]{3,2,1,0:T(4,128)(2,1)S(1)} async-done(((bf16[32,2,4,1792]{3,2,1,0:T(4,128)(2,1)}), bf16[32,2,4,1792]{3,2,1,0:T(4,128)(2,1)S(1)}, u32[]{:S(2)}, u32[]{:S(2)}) %all-to-all-start) | async-done | bytes 917536 | tf_op jit(solution)/shard_map/all_to_all | solution.py:55
  132.7 0.3 fusion.82
  133.0 0.3 reshape_squeeze.7
  133.4 1.8 bitcast_reduce_fusion
  135.1 2.4 fusion.7
  137.6 2.2 fusion.29
  139.8 0.3 reshape_squeeze.6
  140.1 1.7 bitcast_reduce_fusion.1
  141.9 2.4 fusion.5
  144.3 2.2 fusion.35
  146.5 0.3 copy.81
  147.1 0.3 copy.80
  148.4 0.7 copy.74
  149.0 6.4 %all-to-all-start.1 = ((f32[32,2,4,14]{3,2,1,0:T(4,128)}), f32[32,2,4,14]{3,2,1,0:T(4,128)S(1)}, u32[]{:S(2)}, u32[]{:S(2)}) async-start(f32[32,2,4,14]{3,2,1,0:T(4,128)} %copy.74), calls=%async_computation.1 | async-start | bytes 262144 | tf_op jit(solution)/shard_map/all_to_all | solution.py:85
  155.6 1.7 copy.84
  157.2 27.1 %all-to-all-done.1 = f32[32,2,4,14]{3,2,1,0:T(4,128)S(1)} async-done(((f32[32,2,4,14]{3,2,1,0:T(4,128)}), f32[32,2,4,14]{3,2,1,0:T(4,128)S(1)}, u32[]{:S(2)}, u32[]{:S(2)}) %all-to-all-start.1) | async-done | bytes 14368 | tf_op jit(solution)/shard_map/all_to_all | solution.py:85
  184.3 4.8 %all-to-all-start.2 = ((bf16[32,2,4,1792]{3,2,1,0:T(4,128)(2,1)}), bf16[32,2,4,1792]{3,2,1,0:T(4,128)(2,1)S(1)}, u32[]{:S(2)}, u32[]{:S(2)}) async-start(bf16[32,2,4,1792]{3,2,1,0:T(4,128)(2,1)} %copy.84), calls=%async_computation.2 | async-start | bytes 1835008 | tf_op jit(solution)/shard_map/all_to_all | solution.py:82
  189.3 4.6 %fusion.84 = (f32[128,2,7]{2,1,0:T(2,128)S(1)}, f32[128,2,7,64]{3,2,1,0:T(8,128)S(1)}) fusion(bf16[128,2,64,128]{3,2,1,0:T(8,128)(2,1)} %param.15, bf16[128,2,7,128]{3,0,2,1:T(8,128)(2,1)S(1)} %bitcast.103, pred[128,64]{1,0:T(8,128)(4,1)S(1)} %iota_compare_fusion.1), kind=kOutput, calls=%fused_computation.91 | convolution fusion | flops 29702400 | bytes 5127168 | tf_op jit(solution)/shard_map/rhgd,rhtd->rhgt/dot_general | solution.py:100
  194.0 0.8 fusion.40
  194.9 4.5 %fusion.51 = f32[128,2,7,128]{3,2,1,0:T(8,128)} fusion(bf16[128,2,64,128]{3,2,1,0:T(8,128)(2,1)} %param.16, f32[128,2,7,64]{3,2,1,0:T(8,128)S(1)} %get-tuple-element.17, f32[128,2,7]{2,1,0:T(2,128)S(1)} %get-tuple-element.16, pred[128,64]{1,0:T(8,128)(4,1)S(1)} %iota_compare_fusion.1), kind=kOutput, calls=%fused_computation.49 | convolution fusion | flops 29704192 | bytes 5585920 | tf_op jit(solution)/shard_map/rhgt,rhtd->rhgd/dot_general | solution.py:107
  199.5 0.3 fusion.79
  199.8 84.5 %all-to-all-done.2 = bf16[32,2,4,1792]{3,2,1,0:T(4,128)(2,1)S(1)} async-done(((bf16[32,2,4,1792]{3,2,1,0:T(4,128)(2,1)}), bf16[32,2,4,1792]{3,2,1,0:T(4,128)(2,1)S(1)}, u32[]{:S(2)}, u32[]{:S(2)}) %all-to-all-start.2) | async-done | bytes 917536 | tf_op jit(solution)/shard_map/all_to_all | solution.py:82
  284.5 0.5 copy.85
  285.1 3.1 %fusion.25 = bf16[128,2,7,128]{3,0,2,1:T(8,128)(2,1)} fusion(bf16[2,7,128,256]{3,2,1,0:T(8,128)(2,1)S(1)} %bitcast.105, f32[128,2,7,128]{3,2,1,0:T(8,128)} %fusion.51, f32[128,2,7]{0,2,1:T(8,128)S(1)} %get-tuple-element.5, f32[128,2,7]{0,2,1:T(8,128)S(1)} %copy.78, f32[128,2,7]{0,2,1:T(8,128)S(1)} %get-tuple-element.6, ...), kind=kOutput, calls=%fused_computation.28 | convolution fusion | flops 118849536 | bytes 2322944 | tf_op jit(solution)/shard_map/sr,sc->rc/dot_general | solution.py:89
  (32 shorter events, 2.3 us)
Async XLA Ops:
  0.0 133.4 %copy-start.1 = (bf16[2,2,1280,128]{3,2,1,0:T(8,128)(2,1)S(1)}, bf16[2,2,1280,128]{3,2,1,0:T(8,128)(2,1)}, u32[]{:S(2)}) copy-start(bf16[2,2,1280,128]{3,2,1,0:T(8,128)(2,1)} %param.13) | copy-start | bytes 3932164
  4.4 128.4 %all-to-all-start = ((bf16[32,2,4,1792]{3,2,1,0:T(4,128)(2,1)}), bf16[32,2,4,1792]{3,2,1,0:T(4,128)(2,1)S(1)}, u32[]{:S(2)}, u32[]{:S(2)}) async-start(bf16[32,2,4,1792]{3,2,1,0:T(4,128)(2,1)} %reshape.101), calls=%async_computation | async-start | bytes 1835008 | tf_op jit(solution)/shard_map/all_to_all | solution.py:55
  133.4 4.2 %copy-start.3 = (bf16[2,2,1280,128]{3,2,1,0:T(8,128)(2,1)S(1)}, bf16[2,2,1280,128]{3,2,1,0:T(8,128)(2,1)}, u32[]{:S(2)}) copy-start(bf16[2,2,1280,128]{3,2,1,0:T(8,128)(2,1)} %param.14) | copy-start | bytes 3932164
  140.1 4.1 %copy-start.4 = (bf16[2,2,1280,128]{3,2,1,0:T(8,128)(2,1)S(1)}, bf16[2,2,1280,128]{3,2,1,0:T(8,128)(2,1)}, u32[]{:S(2)}) copy-start(bf16[2,2,1280,128]{3,2,1,0:T(8,128)(2,1)} %param.14) | copy-start | bytes 3932164
  146.4 42.7 %copy-start.2 = (s32[128]{0:T(128)S(1)}, s32[128]{0:T(128)}, u32[]{:S(2)}) copy-start(s32[128]{0:T(128)} %param.17) | copy-start | bytes 1540
  146.5 42.8 %copy-start = (bf16[128,14,128]{2,0,1:T(8,128)(2,1)S(1)}, bf16[128,14,128]{2,0,1:T(8,128)(2,1)}, u32[]{:S(2)}) copy-start(bf16[128,14,128]{2,0,1:T(8,128)(2,1)} %param.9) | copy-start | bytes 1376260
  149.0 35.3 %all-to-all-start.1 = ((f32[32,2,4,14]{3,2,1,0:T(4,128)}), f32[32,2,4,14]{3,2,1,0:T(4,128)S(1)}, u32[]{:S(2)}, u32[]{:S(2)}) async-start(f32[32,2,4,14]{3,2,1,0:T(4,128)} %copy.74), calls=%async_computation.1 | async-start | bytes 262144 | tf_op jit(solution)/shard_map/all_to_all | solution.py:85
  184.3 100.0 %all-to-all-start.2 = ((bf16[32,2,4,1792]{3,2,1,0:T(4,128)(2,1)}), bf16[32,2,4,1792]{3,2,1,0:T(4,128)(2,1)S(1)}, u32[]{:S(2)}, u32[]{:S(2)}) async-start(bf16[32,2,4,1792]{3,2,1,0:T(4,128)(2,1)} %copy.84), calls=%async_computation.2 | async-start | bytes 1835008 | tf_op jit(solution)/shard_map/all_to_all | solution.py:82
where the time goes:
time: 291 us; the launch traced here: 288 us
  waiting for transfers between devices  204 us (70%)
  starting transfers between devices  44.5 us (15%)
  matrix products  20.9 us (7%)
  local copies, waits for them, and re-layouts  9.91 us (3%)
  other arithmetic  8.38 us (3%)
    all_to_all x1, waiting for transfers between devices, on_device(): lax.all_to_all(outgoing, 'seq', split_axis=0, concat_axis=0, tiled=True)  92.5 us
    all_to_all x1, waiting for transfers between devices, on_device(): lax.all_to_all(stacked_out.astype(jnp.float32), 'seq', split_axis=0, conc...  84.5 us
    all_to_all x1, starting transfers between devices, on_device(): lax.all_to_all(outgoing, 'seq', split_axis=0, concat_axis=0, tiled=True)  33.2 us
    all_to_all x1, waiting for transfers between devices, on_device(): lax.all_to_all(stacked_lse, 'seq', split_axis=0, concat_axis=0, tiled=True)  27.1 us
    all_to_all x1, starting transfers between devices, on_device(): lax.all_to_all(stacked_lse, 'seq', split_axis=0, concat_axis=0, tiled=True)  6.43 us
  transfers between devices with their start and end apart: 3, of which 3 were waited for; matrix products, arithmetic and copies ran while one was open for 5% of the time, Pallas kernels for 0%

commit v1 on v0

v1 whole, which is shorter than its diff:
```python
import functools
import math

import jax
import jax.numpy as jnp
from jax import lax
from jax.experimental import pallas as pl
from jax.experimental.pallas import tpu as pltpu
from jax.sharding import PartitionSpec as P

NEGATIVE = -1e30
MESH = pl.DeviceIdType.MESH


def weigh(scores, valid):
    scores = jnp.where(valid, scores, NEGATIVE)
    highest = jnp.max(scores, axis=-1, keepdims=True)
    weights = jnp.where(valid, jnp.exp(scores - highest), 0.0)
    total = jnp.sum(weights, axis=-1, keepdims=True)
    return (weights.astype(jnp.bfloat16), total, highest)


def exchange_kernel(
    devices,
    most,
    scale,
    lengths_ref,
    asked_ref,
    keys_hbm,
    values_hbm,
    back_ref,
    back_lse_ref,
    keys,
    values,
    bias,
    incoming,
    answer,
    answer_lse,
    load_sem,
    ask_send,
    ask_recv,
    out_send,
    out_recv,
    lse_send,
    lse_recv,
):
    held, local_kv, tokens, _ = keys_hbm.shape
    slots = held * most
    group = asked_ref.shape[2] // slots
    me = lax.axis_index("seq")
    others = devices - 1

    def place(step):
        half = devices // 2 - (step + 1) // 2
        return half + (step % 2 == 0) * (devices - 2 * half)

    def ask(at):
        return pltpu.make_async_remote_copy(
            src_ref=asked_ref.at[at],
            dst_ref=incoming.at[at],
            send_sem=ask_send.at[at],
            recv_sem=ask_recv.at[at],
            device_id={"seq": (me + at) % devices},
            device_id_type=MESH,
        )

    def reply(at):
        target = {"seq": (me + devices - at) % devices}
        return (
            pltpu.make_async_remote_copy(
                src_ref=answer.at[at],
                dst_ref=back_ref.at[at],
                send_sem=out_send.at[at],
                recv_sem=out_recv.at[at],
                device_id=target,
                device_id_type=MESH,
            ),
            pltpu.make_async_remote_copy(
                src_ref=answer_lse.at[at],
                dst_ref=back_lse_ref.at[at],
                send_sem=lse_send.at[at],
                recv_sem=lse_recv.at[at],
                device_id=target,
                device_id_type=MESH,
            ),
        )

    loads = []
    for image in range(held):
        for head in range(local_kv):
            for number, (source, target) in enumerate(((keys_hbm, keys), (values_hbm, values))):
                loads.append(
                    pltpu.make_async_copy(
                        source.at[image, head],
                        target.at[head, pl.ds(image * tokens, tokens)],
                        load_sem.at[number, image, head],
                    )
                )
    for load in loads:
        load.start()

    barrier = pltpu.get_barrier_semaphore()

    def greet(step, carry):
        pl.semaphore_signal(
            barrier, inc=1, device_id={"seq": (me + 1 + step) % devices}, device_id_type=MESH
        )
        return carry

    lax.fori_loop(0, others, greet, 0)

    row = lax.broadcasted_iota(jnp.int32, (slots, held * tokens), 0)
    token = lax.broadcasted_iota(jnp.int32, (slots, held * tokens), 1)
    valid = jnp.zeros((slots, held * tokens), jnp.bool_)
    for image in range(held):
        mine = (row >= image * most) & (row < (image + 1) * most)
        inside = (token >= image * tokens) & (token < image * tokens + lengths_ref[image])
        valid = valid | (mine & inside)
    bias[...] = jnp.where(valid, 0.0, NEGATIVE)

    pl.semaphore_wait(barrier, others)

    def start_ask(step, carry):
        ask(place(step)).start()
        return carry

    lax.fori_loop(0, others, start_ask, 0)
    for load in loads:
        load.wait()

    lane = lax.broadcasted_iota(jnp.int32, (slots, 128), 1)
    line = lax.broadcasted_iota(jnp.int32, (slots, 128), 0)
    spot = lane - 16 * line

    def attend(read, at, out_to, lse_to):
        packed = jnp.zeros((slots, 128), jnp.float32)
        for head in range(local_kv):
            asked = read[at, head]
            scores = lax.dot_general(
                asked, keys[head], (((1,), (1,)), ((), ())), preferred_element_type=jnp.float32
            )
            scores = scores.reshape(group, slots, held * tokens) * scale + bias[...][None]
            highest = jnp.max(scores, axis=-1, keepdims=True)
            weights = jnp.exp(scores - highest)
            total = jnp.sum(weights, axis=-1, keepdims=True)
            weights = weights.astype(jnp.bfloat16).reshape(group * slots, held * tokens)
            mixed = jnp.dot(weights, values[head], preferred_element_type=jnp.float32)
            mixed = mixed / total.reshape(group * slots, 1)
            out_to[at, head] = mixed.astype(jnp.bfloat16)
            lse = highest + jnp.log(total)
            for member in range(group):
                packed = jnp.where(spot == head * group + member, lse[member], packed)
        lse_to[at] = jnp.sum(packed, axis=0, keepdims=True)

    attend(asked_ref, 0, back_ref, back_lse_ref)

    def serve(step, carry):
        @pl.when(step > 0)
        def _():
            for copy in reply(place(step - 1)):
                copy.start()

        at = place(step)
        ask(at).wait_recv()
        attend(incoming, at, answer, answer_lse)
        return carry

    lax.fori_loop(0, others, serve, 0)
    for copy in reply(place(others - 1)):
        copy.start()

    def finish(step, carry):
        at = place(step)
        ask(at).wait_send()
        for copy in reply(at):
            copy.wait()
        return carry

    lax.fori_loop(0, others, finish, 0)


def exchange(asked, keys, values, lengths, devices, most, scale):
    held, local_kv, tokens, size = keys.shape
    slots = held * most
    message = asked.shape[1:]
    vmem = pl.BlockSpec(memory_space=pltpu.VMEM)
    return pl.pallas_call(
        functools.partial(exchange_kernel, devices, most, scale),
        out_shape=(
            jax.ShapeDtypeStruct(asked.shape, jnp.bfloat16),
            jax.ShapeDtypeStruct((devices, 1, 128), jnp.float32),
        ),
        in_specs=[
            pl.BlockSpec(memory_space=pltpu.SMEM),
            vmem,
            pl.BlockSpec(memory_space=pl.ANY),
            pl.BlockSpec(memory_space=pl.ANY),
        ],
        out_specs=(vmem, vmem),
        scratch_shapes=[
            pltpu.VMEM((local_kv, held * tokens, size), jnp.bfloat16),
            pltpu.VMEM((local_kv, held * tokens, size), jnp.bfloat16),
            pltpu.VMEM((slots, held * tokens), jnp.float32),
            pltpu.VMEM((devices, *message), jnp.bfloat16),
            pltpu.VMEM((devices, *message), jnp.bfloat16),
            pltpu.VMEM((devices, 1, 128), jnp.float32),
            pltpu.SemaphoreType.DMA((2, held, local_kv)),
            pltpu.SemaphoreType.DMA((devices,)),
            pltpu.SemaphoreType.DMA((devices,)),
            pltpu.SemaphoreType.DMA((devices,)),
            pltpu.SemaphoreType.DMA((devices,)),
            pltpu.SemaphoreType.DMA((devices,)),
            pltpu.SemaphoreType.DMA((devices,)),
        ],
        compiler_params=pltpu.CompilerParams(
            collective_id=0, has_side_effects=True, vmem_limit_bytes=40 * 1024 * 1024
        ),
    )(lengths, asked, keys, values)


def on_device(
    queries,
    request_image,
    image_slot,
    image_lengths,
    image_keys,
    image_values,
    text_keys,
    text_values,
    text_lengths,
):
    rows, local_heads, head_size = queries.shape
    local_kv = image_keys.shape[1]
    group = local_heads // local_kv
    images = image_slot.shape[0]
    held = image_keys.shape[0]
    text_tokens = text_keys.shape[2]
    devices = lax.axis_size("seq")
    most = max(2, 2 * rows // images)
    slots_each = held * most
    scale = 1.0 / math.sqrt(head_size)
    me = lax.axis_index("seq")
    image_ids = jnp.arange(images, dtype=jnp.int32)
    chosen = request_image == image_ids[None, :]
    slots = jnp.sum(jnp.where(chosen, image_slot[None, :], 0), axis=1)
    slots = (slots + (devices - me) * held) % images
    slot_hits = (slots[:, None] == image_ids[None, :]).astype(jnp.int32)
    ranks = jnp.sum(slot_hits * (jnp.cumsum(slot_hits, axis=0) - 1), axis=1)
    targets = slots * most + ranks
    dispatch = (jnp.arange(images * most, dtype=jnp.int32)[:, None] == targets[None, :]).astype(
        jnp.bfloat16
    )
    by_head = queries.transpose(1, 0, 2)
    asked = jnp.einsum("sr,hrd->hsd", dispatch, by_head, preferred_element_type=jnp.float32)
    asked = asked.astype(jnp.bfloat16).reshape(local_heads, devices, slots_each, head_size)
    asked = asked.transpose(1, 0, 2, 3).reshape(devices, local_kv, group * slots_each, head_size)
    back, back_lse = exchange(asked, image_keys, image_values, image_lengths, devices, most, scale)
    back = back.reshape(devices, local_heads, slots_each, head_size).transpose(1, 0, 2, 3)
    back = back.reshape(local_heads, images * most, head_size)
    image_part = jnp.einsum("sr,hsd->rhd", dispatch, back, preferred_element_type=jnp.float32)
    image_part = image_part.reshape(rows, local_kv, group, head_size)
    back_lse = back_lse.reshape(devices * slots_each, 16)[:, :local_heads]
    image_lse = jnp.einsum(
        "sr,sc->rc", dispatch.astype(jnp.float32), back_lse, precision=lax.Precision.HIGHEST
    )
    image_lse = image_lse.reshape(rows, local_kv, group)
    heads = queries.reshape(rows, local_kv, group, head_size)
    scores = (
        jnp.einsum("rhgd,rhtd->rhgt", heads, text_keys, preferred_element_type=jnp.float32) * scale
    )
    valid = (jnp.arange(text_tokens, dtype=jnp.int32)[None, :] < text_lengths[:, None])[
        :, None, None, :
    ]
    weights, total, highest = weigh(scores, valid)
    text_out = (
        jnp.einsum("rhgt,rhtd->rhgd", weights, text_values, preferred_element_type=jnp.float32)
        / total
    )
    text_lse = highest[..., 0] + jnp.log(total[..., 0])
    upper = jnp.maximum(image_lse, text_lse)
    image_weight = jnp.exp(image_lse - upper)[..., None]
    text_weight = jnp.exp(text_lse - upper)[..., None]
    merged = (image_weight * image_part + text_weight * text_out) / (image_weight + text_weight)
    return merged.reshape(rows, local_heads, head_size).astype(jnp.bfloat16)


def solution(mesh):
    in_specs = (
        P(("groups", "seq"), "head", None),
        P(("groups", "seq"), None),
        P("groups"),
        P(("groups", "seq")),
        P(("groups", "seq"), "head", None, None),
        P(("groups", "seq"), "head", None, None),
        P(("groups", "seq"), "head", None, None),
        P(("groups", "seq"), "head", None, None),
        P(("groups", "seq")),
    )
    out_specs = P(("groups", "seq"), "head", None)
    return jax.shard_map(
        on_device, mesh=mesh, in_specs=in_specs, out_specs=out_specs, check_vma=False
    )
```

time: 291 us -> 214 us (0.74)
  waiting for transfers between devices: 204 us -> 0 us
  Pallas kernels: 0 us -> 195 us
  starting transfers between devices: 44.5 us -> 0 us
  matrix products: 20.9 us -> 12.7 us
  local copies, waits for them, and re-layouts: 9.91 us -> 2.51 us
  other arithmetic: 8.38 us -> 3.73 us
    all_to_all x3 -> x0, waiting for transfers between devices: 204 us -> none  [the longest x1 92.5 us: on_device(): lax.all_to_all(outgoing, 'seq', split_axis=0, concat_axis=0, tiled=True)]
    pallas_call x0 -> x1, Pallas kernels: none -> 195 us  [exchange(): pl.pallas_call(functools.partial(exchange_kernel, devices, most, scale),...]
    all_to_all x3 -> x0, starting transfers between devices: 44.5 us -> none  [the longest x1 33.2 us: on_device(): lax.all_to_all(outgoing, 'seq', split_axis=0, concat_axis=0, tiled=True)]
    dot_general x7 -> x3, matrix products: 11.8 us -> 4.47 us  [the longest x1 1.98 us: on_device(): jnp.einsum('sr,hsd->rhd', dispatch, back, preferred_element_type=jnp.floa...]
    reduce_sum x3 -> x1, other arithmetic: 5.61 us -> 0.81 us  [weigh(): total = jnp.sum(weights, axis=-1, keepdims=True)]
  transfers between devices with their start and end apart: 3 -> 0, of which waited for: 3 -> 0; matrix products, arithmetic and copies ran while one was open for 5% -> 0% of each run, Pallas kernels for 0% -> 0%
where the time goes in v1:
time: 214 us
  Pallas kernels  195 us (91%)
  matrix products  12.7 us (6%)
  other arithmetic  3.73 us (2%)
  local copies, waits for them, and re-layouts  2.51 us (1%)
    pallas_call x1, Pallas kernels, exchange(): pl.pallas_call(functools.partial(exchange_kernel, devices, most, scale),...  195 us
    dot_general x1, matrix products, on_device(): jnp.einsum('rhgd,rhtd->rhgt', heads, text_keys, preferred_element_type=jn...  4.78 us

profile of v1, /device:TPU:37, one launch (start us, length us, event | category | flops | bytes accessed | tf_op | source)
XLA Modules:
  0.0 213.8 jit_solution(13479263310399718567)
XLA Ops:
  0.0 0.0 copy-start
  0.0 0.0 copy-start.1
  0.0 1.0 select_reduce_fusion.1
  1.0 0.1 fusion.24
  1.1 0.2 reduce_window_sum.11
  1.3 0.2 select_reduce_fusion
  1.5 0.0 copy-start.3
  1.5 0.6 copy-done.3
  2.1 1.5 fusion.1
  3.6 0.2 copy.35
  3.8 0.0 copy-done
  3.8 0.0 copy-done.1
  3.8 0.0 copy-start.2
  3.8 0.6 copy-done.2
  4.5 194.7 %shard_map.91 = (bf16[32,2,56,128]{3,2,1,0:T(8,128)(2,1)S(1)}, f32[32,1,128]{2,1,0:T(1,128)S(1)}) custom-call(s32[2]{0:T(128)S(1)} %copy-done.2, bf16[32,2,56,128]{3,2,1,0:T(8,128)(2,1)S(1)} %bitcast.34, bf16[2,2,1280,128]{3,2,1,0:T(8,128)(2,1)S(1)} %copy-done, bf16[2,2,1280,128]{3,2,1,0:T(8,128)(2,1)S(1)} %copy-done.1), custom_call_target="tpu_custom_call" | custom-call | tf_op jit(solution)/shard_map/pallas_call | solution.py:187
  199.2 0.5 broadcast.81
  199.7 0.7 reduce.3
  200.4 0.1 reshape.115
  200.5 1.0 fusion.15
  201.5 0.7 iota_compare_fusion.2
  202.2 4.8 %fusion.32 = (f32[128,2,7]{2,1,0:T(2,128)S(1)}, f32[128,2,7,64]{3,2,1,0:T(8,128)S(1)}) fusion(bf16[128,2,64,128]{3,2,1,0:T(8,128)(2,1)} %param.15, bf16[128,2,7,128]{3,0,2,1:T(8,128)(2,1)} %bitcast.36, pred[128,64]{1,0:T(8,128)(4,1)S(1)} %iota_compare_fusion.2), kind=kOutput, calls=%fused_computation.45 | convolution fusion | flops 29702400 | bytes 5127168 | tf_op jit(solution)/shard_map/rhgd,rhtd->rhgt/dot_general | solution.py:269
  207.0 0.8 fusion.7
  207.8 0.1 copy.37
  207.9 0.1 copy.38
  208.1 0.1 copy.45
  208.1 0.2 copy.42
  208.4 0.0 copy-start.4
  208.4 3.4 %fusion.8 = f32[128,2,7,128]{3,2,1,0:T(8,128)S(1)} fusion(bf16[128,2,64,128]{3,2,1,0:T(8,128)(2,1)} %param.16, f32[128,2,7,64]{3,2,1,0:T(8,128)S(1)} %get-tuple-element.13, f32[128,2,7]{2,1,0:T(2,128)S(1)} %get-tuple-element.12, pred[128,64]{1,0:T(8,128)(4,1)S(1)} %iota_compare_fusion.2), kind=kOutput, calls=%fused_computation.13 | convolution fusion | flops 29704192 | bytes 5585920 | tf_op jit(solution)/shard_map/rhgt,rhtd->rhgd/dot_general | solution.py:276
  211.8 0.0 copy-done.4
  211.8 2.0 fusion.4
  (7 shorter events, 0.1 us)
Async XLA Ops:
  0.0 3.8 %copy-start = (bf16[2,2,1280,128]{3,2,1,0:T(8,128)(2,1)S(1)}, bf16[2,2,1280,128]{3,2,1,0:T(8,128)(2,1)}, u32[]{:S(2)}) copy-start(bf16[2,2,1280,128]{3,2,1,0:T(8,128)(2,1)} %keys_hbm.1) | copy-start | bytes 3932164
  0.0 3.8 %copy-start.1 = (bf16[2,2,1280,128]{3,2,1,0:T(8,128)(2,1)S(1)}, bf16[2,2,1280,128]{3,2,1,0:T(8,128)(2,1)}, u32[]{:S(2)}) copy-start(bf16[2,2,1280,128]{3,2,1,0:T(8,128)(2,1)} %values_hbm.1) | copy-start | bytes 3932164
  1.5 0.6 copy-start.3
  3.8 0.7 copy-start.2
  208.4 3.4 %copy-start.4 = (s32[128]{0:T(128)S(1)}, s32[128]{0:T(128)}, u32[]{:S(2)}) copy-start(s32[128]{0:T(128)} %copy-done.3) | copy-start | bytes 1540

commit v2 on v1

v2 whole, which is shorter than its diff:
```python
import functools
import math

import jax
import jax.numpy as jnp
from jax import lax
from jax.experimental import pallas as pl
from jax.experimental.pallas import tpu as pltpu
from jax.sharding import PartitionSpec as P

NEGATIVE = -1e30
MESH = pl.DeviceIdType.MESH
CHUNK = 16


def iota(shape, axis):
    return lax.broadcasted_iota(jnp.int32, shape, axis).astype(jnp.float32)


def column(line):
    size = line.shape[1]
    same = iota((size, size), 0) == iota((size, size), 1)
    return jnp.sum(jnp.where(same, line, 0.0), axis=1, keepdims=True)


def kernel(
    devices,
    most,
    scale,
    lengths_ref,
    named_ref,
    slot_ref,
    text_lengths_ref,
    queries_hbm,
    image_keys_hbm,
    image_values_hbm,
    text_keys_hbm,
    text_values_hbm,
    out_ref,
    queries,
    keys,
    values,
    text_keys,
    text_values,
    bias,
    pick,
    asked,
    incoming,
    answer,
    answer_lse,
    back,
    back_lse,
    text_out,
    text_lse,
    query_sem,
    load_sem,
    text_sem,
    ask_send,
    ask_recv,
    out_send,
    out_recv,
    lse_send,
    lse_recv,
):
    held, local_kv, tokens, size = image_keys_hbm.shape
    heads, rows, _ = queries_hbm.shape
    text_tokens = text_keys_hbm.shape[2]
    images = slot_ref.shape[1]
    slots = held * most
    group = heads // local_kv
    me = lax.axis_index("seq")
    others = devices - 1

    def place(step):
        half = devices // 2 - (step + 1) // 2
        return half + (step % 2 == 0) * (devices - 2 * half)

    def ask(at):
        return pltpu.make_async_remote_copy(
            src_ref=asked.at[at],
            dst_ref=incoming.at[at],
            send_sem=ask_send.at[at],
            recv_sem=ask_recv.at[at],
            device_id={"seq": (me + at) % devices},
            device_id_type=MESH,
        )

    def reply(at):
        target = {"seq": (me + devices - at) % devices}
        return (
            pltpu.make_async_remote_copy(
                src_ref=answer.at[at],
                dst_ref=back.at[at],
                send_sem=out_send.at[at],
                recv_sem=out_recv.at[at],
                device_id=target,
                device_id_type=MESH,
            ),
            pltpu.make_async_remote_copy(
                src_ref=answer_lse.at[at],
                dst_ref=back_lse.at[at],
                send_sem=lse_send.at[at],
                recv_sem=lse_recv.at[at],
                device_id=target,
                device_id_type=MESH,
            ),
        )

    barrier = pltpu.get_barrier_semaphore()

    def greet(step, carry):
        pl.semaphore_signal(
            barrier, inc=1, device_id={"seq": (me + 1 + step) % devices}, device_id_type=MESH
        )
        return carry

    lax.fori_loop(0, others, greet, 0)

    first = pltpu.make_async_copy(queries_hbm, queries, query_sem)
    first.start()
    loads = []
    for image in range(held):
        for head in range(local_kv):
            for number, (source, target) in enumerate(
                ((image_keys_hbm, keys), (image_values_hbm, values))
            ):
                loads.append(
                    pltpu.make_async_copy(
                        source.at[image, head],
                        target.at[head, pl.ds(image * tokens, tokens)],
                        load_sem.at[number, image, head],
                    )
                )
    loads.append(pltpu.make_async_copy(text_keys_hbm, text_keys, text_sem.at[0]))
    loads.append(pltpu.make_async_copy(text_values_hbm, text_values, text_sem.at[1]))
    for load in loads:
        load.start()

    named = named_ref[...].astype(jnp.float32)
    slot_column = column(slot_ref[...].astype(jnp.float32))
    slot_of = jnp.where(iota((images, rows), 0) == named, slot_column, 0.0)
    slot_of = jnp.sum(slot_of, axis=0, keepdims=True)
    near = slot_of + ((devices - me) * held).astype(jnp.float32)
    near = jnp.where(near >= images, near - images, near)
    near_column = column(near)
    same = near_column == near
    earlier = iota((rows, rows), 0) < iota((rows, rows), 1)
    rank = jnp.sum(jnp.where(same & earlier, 1.0, 0.0), axis=0, keepdims=True)
    target_row = near * most + rank
    target = column(target_row)
    place_in = jnp.where(iota((images * most, rows), 0) == target_row, 1.0, 0.0)
    place_in = place_in.astype(jnp.bfloat16)
    pick[...] = jnp.where(iota((rows, images * most), 1) == target, 1.0, 0.0).astype(jnp.bfloat16)
    first.wait()
    for head in range(heads):
        sent = jnp.dot(place_in, queries[head], preferred_element_type=jnp.float32)
        sent = sent.reshape(devices, slots, size).astype(jnp.bfloat16)
        asked[:, head // group, pl.ds(head % group * slots, slots), :] = sent

    row = lax.broadcasted_iota(jnp.int32, (slots, held * tokens), 0)
    token = lax.broadcasted_iota(jnp.int32, (slots, held * tokens), 1)
    valid = jnp.zeros((slots, held * tokens), jnp.bool_)
    for image in range(held):
        mine = (row >= image * most) & (row < (image + 1) * most)
        inside = (token >= image * tokens) & (token < image * tokens + lengths_ref[image])
        valid = valid | (mine & inside)
    bias[...] = jnp.where(valid, 0.0, NEGATIVE)

    pl.semaphore_wait(barrier, others)

    def start_ask(step, carry):
        ask(place(step)).start()
        return carry

    lax.fori_loop(0, others, start_ask, 0)
    for load in loads:
        load.wait()

    text_length = column(text_lengths_ref[...].astype(jnp.float32))
    text_lse[...] = jnp.broadcast_to(text_length, text_lse.shape)
    wide = CHUNK * text_tokens
    lane = lax.broadcasted_iota(jnp.int32, (CHUNK, 128), 1)

    def read_text(chunk, carry):
        start = pl.multiple_of(chunk * CHUNK, CHUNK)
        limit = text_lse[pl.ds(start, CHUNK), :][:, :1]
        ahead = iota((CHUNK, wide), 1) - iota((CHUNK, wide), 0) * text_tokens
        text_bias = jnp.where((ahead >= 0) & (ahead < limit), 0.0, NEGATIVE)
        packed = jnp.zeros((CHUNK, 128), jnp.float32)
        for kv in range(local_kv):
            asking = queries[kv * group : (kv + 1) * group, pl.ds(start, CHUNK), :]
            asking = asking.reshape(group * CHUNK, size)
            those = text_keys[pl.ds(start, CHUNK), kv].reshape(wide, size)
            scores = lax.dot_general(
                asking, those, (((1,), (1,)), ((), ())), preferred_element_type=jnp.float32
            )
            scores = scores.reshape(group, CHUNK, wide) * scale + text_bias[None]
            highest = jnp.max(scores, axis=-1, keepdims=True)
            weights = jnp.exp(scores - highest)
            total = jnp.sum(weights, axis=-1, keepdims=True)
            weights = weights.astype(jnp.bfloat16).reshape(group * CHUNK, wide)
            those = text_values[pl.ds(start, CHUNK), kv].reshape(wide, size)
            mixed = jnp.dot(weights, those, preferred_element_type=jnp.float32)
            mixed = mixed.reshape(group, CHUNK, size) / total
            text_out[kv * group : (kv + 1) * group, pl.ds(start, CHUNK), :] = mixed
            lse = highest + jnp.log(total)
            for member in range(group):
                packed = jnp.where(lane == kv * group + member, lse[member], packed)
        text_lse[pl.ds(start, CHUNK), :] = packed
        return carry

    lax.fori_loop(0, rows // CHUNK, read_text, 0)

    spot = lax.broadcasted_iota(jnp.int32, (slots, 128), 1) - 16 * lax.broadcasted_iota(
        jnp.int32, (slots, 128), 0
    )

    def attend(read, at, out_to, lse_to):
        packed = jnp.zeros((slots, 128), jnp.float32)
        for head in range(local_kv):
            scores = lax.dot_general(
                read[at, head],
                keys[head],
                (((1,), (1,)), ((), ())),
                preferred_element_type=jnp.float32,
            )
            scores = scores.reshape(group, slots, held * tokens) * scale + bias[...][None]
            highest = jnp.max(scores, axis=-1, keepdims=True)
            weights = jnp.exp(scores - highest)
            total = jnp.sum(weights, axis=-1, keepdims=True)
            weights = weights.astype(jnp.bfloat16).reshape(group * slots, held * tokens)
            mixed = jnp.dot(weights, values[head], preferred_element_type=jnp.float32)
            mixed = mixed / total.reshape(group * slots, 1)
            out_to[at, head] = mixed.astype(jnp.bfloat16)
            lse = highest + jnp.log(total)
            for member in range(group):
                packed = jnp.where(spot == head * group + member, lse[member], packed)
        lse_to[at] = jnp.sum(packed, axis=0, keepdims=True)

    attend(asked, 0, back, back_lse)

    def serve(step, carry):
        @pl.when(step > 0)
        def _():
            for copy in reply(place(step - 1)):
                copy.start()

        at = place(step)
        ask(at).wait_recv()
        attend(incoming, at, answer, answer_lse)
        return carry

    lax.fori_loop(0, others, serve, 0)
    for copy in reply(place(others - 1)):
        copy.start()

    def finish(step, carry):
        at = place(step)
        ask(at).wait_send()
        for copy in reply(at):
            copy.wait()
        return carry

    lax.fori_loop(0, others, finish, 0)

    target = column(target_row)
    from_at = iota((rows, devices), 1) * slots
    from_here = jnp.where((target >= from_at) & (target < from_at + slots), 1.0, 0.0)
    chosen = jnp.dot(
        from_here,
        back_lse[...].reshape(devices, 128),
        precision=lax.Precision.HIGHEST,
        preferred_element_type=jnp.float32,
    )
    offset = jnp.sum(from_here * from_at, axis=1, keepdims=True)
    start = (target - offset) * 16
    lanes = iota((rows, 128), 1)
    chosen = jnp.where((lanes >= start) & (lanes < start + 16), chosen, 0.0)
    fold = iota((128, 128), 0) - iota((128, 128), 1)
    landed = jnp.zeros((128, 128), jnp.float32)
    for line in range(slots):
        landed = jnp.where(fold == 16 * line, 1.0, landed)
    landed = jnp.where(iota((128, 128), 1) < 16, landed, 0.0)
    image_lse = jnp.dot(
        chosen, landed, precision=lax.Precision.HIGHEST, preferred_element_type=jnp.float32
    )
    top = jnp.maximum(image_lse, text_lse[...])
    image_weight = jnp.exp(image_lse - top)
    text_weight = jnp.exp(text_lse[...] - top)
    whole = image_weight + text_weight
    for head in range(heads):
        came = back[:, head // group, pl.ds(head % group * slots, slots), :]
        came = came.astype(jnp.float32).reshape(devices * slots, size).astype(jnp.bfloat16)
        image_out = jnp.dot(pick[...], came, preferred_element_type=jnp.float32)
        merged = image_weight[:, head : head + 1] * image_out
        merged = merged + text_weight[:, head : head + 1] * text_out[head]
        out_ref[head] = (merged / whole[:, head : head + 1]).astype(jnp.bfloat16)


def on_device(
    queries,
    request_image,
    image_slot,
    image_lengths,
    image_keys,
    image_values,
    text_keys,
    text_values,
    text_lengths,
):
    rows, heads, size = queries.shape
    held, local_kv, tokens, _ = image_keys.shape
    images = image_slot.shape[0]
    devices = lax.axis_size("seq")
    most = max(2, 2 * rows // images)
    slots = held * most
    scale = 1.0 / math.sqrt(size)
    message = (devices, local_kv, heads // local_kv * slots, size)
    vmem = pl.BlockSpec(memory_space=pltpu.VMEM)
    hbm = pl.BlockSpec(memory_space=pl.ANY)
    links = pltpu.SemaphoreType.DMA((devices,))
    out = pl.pallas_call(
        functools.partial(kernel, devices, most, scale),
        out_shape=jax.ShapeDtypeStruct((heads, rows, size), jnp.bfloat16),
        in_specs=[pl.BlockSpec(memory_space=pltpu.SMEM), vmem, vmem, vmem, hbm, hbm, hbm, hbm, hbm],
        out_specs=vmem,
        scratch_shapes=[
            pltpu.VMEM((heads, rows, size), jnp.bfloat16),
            pltpu.VMEM((local_kv, held * tokens, size), jnp.bfloat16),
            pltpu.VMEM((local_kv, held * tokens, size), jnp.bfloat16),
            pltpu.VMEM(text_keys.shape, jnp.bfloat16),
            pltpu.VMEM(text_values.shape, jnp.bfloat16),
            pltpu.VMEM((slots, held * tokens), jnp.float32),
            pltpu.VMEM((rows, images * most), jnp.bfloat16),
            pltpu.VMEM(message, jnp.bfloat16),
            pltpu.VMEM(message, jnp.bfloat16),
            pltpu.VMEM(message, jnp.bfloat16),
            pltpu.VMEM((devices, 1, 128), jnp.float32),
            pltpu.VMEM(message, jnp.bfloat16),
            pltpu.VMEM((devices, 1, 128), jnp.float32),
            pltpu.VMEM((heads, rows, size), jnp.float32),
            pltpu.VMEM((rows, 128), jnp.float32),
            pltpu.SemaphoreType.DMA,
            pltpu.SemaphoreType.DMA((2, held, local_kv)),
            pltpu.SemaphoreType.DMA((2,)),
            links,
            links,
            links,
            links,
            links,
            links,
        ],
        compiler_params=pltpu.CompilerParams(
            collective_id=0, has_side_effects=True, vmem_limit_bytes=62 * 1024 * 1024
        ),
    )(
        image_lengths,
        request_image.reshape(1, rows),
        image_slot.reshape(1, images),
        text_lengths.reshape(1, rows),
        queries.transpose(1, 0, 2),
        image_keys,
        image_values,
        text_keys,
        text_values,
    )
    return out.transpose(1, 0, 2)


def solution(mesh):
    in_specs = (
        P(("groups", "seq"), "head", None),
        P(("groups", "seq"), None),
        P("groups"),
        P(("groups", "seq")),
        P(("groups", "seq"), "head", None, None),
        P(("groups", "seq"), "head", None, None),
        P(("groups", "seq"), "head", None, None),
        P(("groups", "seq"), "head", None, None),
        P(("groups", "seq")),
    )
    out_specs = P(("groups", "seq"), "head", None)
    return jax.shard_map(
        on_device, mesh=mesh, in_specs=in_specs, out_specs=out_specs, check_vma=False
    )
```

time: 214 us -> 199 us (0.930)
  matrix products: 12.7 us -> 0 us
  other arithmetic: 3.73 us -> 0 us
    dot_general x5 -> x0, matrix products: 12.7 us -> none  [the longest x1 4.78 us: on_device(): jnp.einsum('rhgd,rhtd->rhgt', heads, text_keys, preferred_element_type=jn...]
where the time goes in v2:
time: 199 us; the launch traced here: 198 us
  Pallas kernels  196 us (98%)
    pallas_call x1, Pallas kernels, on_device(): pl.pallas_call(functools.partial(kernel, devices, most, scale), out_shape...  196 us

profile of v2, /device:TPU:37, one launch (start us, length us, event | category | flops | bytes accessed | tf_op | source)
XLA Modules:
  0.0 198.1 jit_solution(7234427094636276594)
XLA Ops:
  0.0 196.3 %shard_map.91 = bf16[14,128,128]{2,1,0:T(8,128)(2,1)} custom-call(s32[2]{0:T(128)} %lengths_ref.1, s32[1,128]{1,0:T(1,128)} %bitcast.7, s32[1,64]{1,0:T(1,128)} %bitcast.8, s32[1,128]{1,0:T(1,128)} %bitcast.9, bf16[14,128,128]{2,1,0:T(8,128)(2,1)} %bitcast.6, bf16[2,2,1280,128]{3,2,1,0:T(8,128)(2,1)} %image_keys_hbm.1, ...), custom_call_target="tpu_custom_call" | custom-call | tf_op jit(solution)/shard_map/pallas_call | solution.py:322
  196.3 1.8 copy.11

commit v3 on v2

--- a/solution.py
+++ b/solution.py
@@ -52,6 +52,7 @@
     back_lse,
     text_out,
     text_lse,
+    far_sem,
     query_sem,
     load_sem,
     text_sem,
@@ -71,9 +72,16 @@
     me = lax.axis_index("seq")
     others = devices - 1
 
-    def place(step):
-        half = devices // 2 - (step + 1) // 2
-        return half + (step % 2 == 0) * (devices - 2 * half)
+    reach = devices // 4
+    close = 2 * reach
+
+    def near_place(step):
+        hops = reach - step // 2
+        return hops + (step % 2) * (devices - 2 * hops)
+
+    def far_place(step):
+        hops = devices // 2 - (step + 1) // 2
+        return hops + (1 - step % 2) * (devices - 2 * hops)
 
     def ask(at):
         return pltpu.make_async_remote_copy(
@@ -110,11 +118,14 @@
 
     def greet(step, carry):
         pl.semaphore_signal(
-            barrier, inc=1, device_id={"seq": (me + 1 + step) % devices}, device_id_type=MESH
+            barrier,
+            inc=1,
+            device_id={"seq": (me + near_place(step)) % devices},
+            device_id_type=MESH,
         )
         return carry
 
-    lax.fori_loop(0, others, greet, 0)
+    lax.fori_loop(0, close, greet, 0)
 
     first = pltpu.make_async_copy(queries_hbm, queries, query_sem)
     first.start()
@@ -166,13 +177,20 @@
         valid = valid | (mine & inside)
     bias[...] = jnp.where(valid, 0.0, NEGATIVE)
 
-    pl.semaphore_wait(barrier, others)
-
-    def start_ask(step, carry):
-        ask(place(step)).start()
-        return carry
-
-    lax.fori_loop(0, others, start_ask, 0)
+    pl.semaphore_wait(barrier, close)
+    for step in range(2):
+        pl.semaphore_signal(
+            far_sem,
+            inc=1,
+            device_id={"seq": (me + near_place(step)) % devices},
+            device_id_type=MESH,
+        )
+
+    def ask_near(step, carry):
+        ask(near_place(step)).start()
+        return carry
+
+    lax.fori_loop(0, close, ask_near, 0)
     for load in loads:
         load.wait()
 
@@ -210,6 +228,13 @@
         return carry
 
     lax.fori_loop(0, rows // CHUNK, read_text, 0)
+    pl.semaphore_wait(far_sem, 2)
+
+    def ask_far(step, carry):
+        ask(far_place(step)).start()
+        return carry
+
+    lax.fori_loop(0, others - close, ask_far, 0)
 
     spot = lax.broadcasted_iota(jnp.int32, (slots, 128), 1) - 16 * lax.broadcasted_iota(
         jnp.int32, (slots, 128), 0
@@ -239,29 +264,42 @@
 
     attend(asked, 0, back, back_lse)
 
-    def serve(step, carry):
+    def serve(at):
+        ask(at).wait_recv()
+        attend(incoming, at, answer, answer_lse)
+
+    def send_back(at):
+        for copy in reply(at):
+            copy.start()
+
+    def serve_near(step, carry):
+        serve(near_place(step))
+        return carry
+
+    def serve_far(step, carry):
         @pl.when(step > 0)
         def _():
-            for copy in reply(place(step - 1)):
-                copy.start()
-
-        at = place(step)
-        ask(at).wait_recv()
-        attend(incoming, at, answer, answer_lse)
-        return carry
-
-    lax.fori_loop(0, others, serve, 0)
-    for copy in reply(place(others - 1)):
-        copy.start()
+            send_back(far_place(step - 1))
+
+        serve(far_place(step))
+        return carry
+
+    def send_near(step, carry):
+        send_back(near_place(step))
+        return carry
+
+    lax.fori_loop(0, close, serve_near, 0)
+    lax.fori_loop(0, others - close, serve_far, 0)
+    send_back(far_place(others - close - 1))
+    lax.fori_loop(0, close, send_near, 0)
 
     def finish(step, carry):
-        at = place(step)
-        ask(at).wait_send()
-        for copy in reply(at):
+        ask(step).wait_send()
+        for copy in reply(step):
             copy.wait()
         return carry
 
-    lax.fori_loop(0, others, finish, 0)
+    lax.fori_loop(1, devices, finish, 0)
 
     target = column(target_row)
     from_at = iota((rows, devices), 1) * slots
@@ -340,6 +378,7 @@
             pltpu.VMEM((devices, 1, 128), jnp.float32),
             pltpu.VMEM((heads, rows, size), jnp.float32),
             pltpu.VMEM((rows, 128), jnp.float32),
+            pltpu.SemaphoreType.REGULAR,
             pltpu.SemaphoreType.DMA,
             pltpu.SemaphoreType.DMA((2, held, local_kv)),
             pltpu.SemaphoreType.DMA((2,)),

time: 199 us -> 195 us (0.980)
  Pallas kernels: 196 us -> 193 us
    pallas_call x1, Pallas kernels: 196 us -> 193 us  [on_device(): pl.pallas_call(functools.partial(kernel, devices, most, scale), out_shape...]
where the time goes in v3:
time: 195 us; the launch traced here: 194 us
  Pallas kernels  193 us (99%)
    pallas_call x1, Pallas kernels, on_device(): pl.pallas_call(functools.partial(kernel, devices, most, scale), out_shape...  193 us

profile of v3, /device:TPU:37, one launch (start us, length us, event | category | flops | bytes accessed | tf_op | source)
XLA Modules:
  0.0 194.4 jit_solution(9927002019092722960)
XLA Ops:
  0.0 192.6 %shard_map.91 = bf16[14,128,128]{2,1,0:T(8,128)(2,1)} custom-call(s32[2]{0:T(128)} %lengths_ref.1, s32[1,128]{1,0:T(1,128)} %bitcast.7, s32[1,64]{1,0:T(1,128)} %bitcast.8, s32[1,128]{1,0:T(1,128)} %bitcast.9, bf16[14,128,128]{2,1,0:T(8,128)(2,1)} %bitcast.6, bf16[2,2,1280,128]{3,2,1,0:T(8,128)(2,1)} %image_keys_hbm.1, ...), custom_call_target="tpu_custom_call" | custom-call | tf_op jit(solution)/shard_map/pallas_call | solution.py:360
  192.6 1.8 copy.11

commit v4 on v3

--- a/solution.py
+++ b/solution.py
@@ -27,16 +27,20 @@
     devices,
     most,
     scale,
-    lengths_ref,
-    named_ref,
-    slot_ref,
-    text_lengths_ref,
+    lengths_hbm,
+    named_hbm,
+    slot_hbm,
+    text_lengths_hbm,
     queries_hbm,
     image_keys_hbm,
     image_values_hbm,
     text_keys_hbm,
     text_values_hbm,
     out_ref,
+    lengths_ref,
+    named_ref,
+    slot_ref,
+    text_lengths_ref,
     queries,
     keys,
     values,
@@ -53,7 +57,7 @@
     text_out,
     text_lse,
     far_sem,
-    query_sem,
+    first_sem,
     load_sem,
     text_sem,
     ask_send,
@@ -66,7 +70,7 @@
     held, local_kv, tokens, size = image_keys_hbm.shape
     heads, rows, _ = queries_hbm.shape
     text_tokens = text_keys_hbm.shape[2]
-    images = slot_ref.shape[1]
+    images = slot_hbm.shape[1]
     slots = held * most
     group = heads // local_kv
     me = lax.axis_index("seq")
@@ -74,10 +78,20 @@
 
     reach = devices // 4
     close = 2 * reach
+    stages = [(0, 2)]
+    while stages[-1][1] < reach:
+        stages.append((stages[-1][1], 2 * stages[-1][1]))
+
+    def both(hops, step):
+        return hops + (step % 2) * (devices - 2 * hops)
 
     def near_place(step):
-        hops = reach - step // 2
-        return hops + (step % 2) * (devices - 2 * hops)
+        turn = step // 2
+        hops, before = -turn, 0
+        for low, high in stages:
+            hops = hops + (turn >= low) * (low + high - before)
+            before = low + high
+        return both(hops, step)
 
     def far_place(step):
         hops = devices // 2 - (step + 1) // 2
@@ -114,21 +128,30 @@
             ),
         )
 
+    def signal(sem, hops):
+        for at in (hops, devices - hops):
+            pl.semaphore_signal(
+                sem, inc=1, device_id={"seq": (me + at) % devices}, device_id_type=MESH
+            )
+
+    first = [
+        pltpu.make_async_copy(source, target, first_sem.at[number])
+        for number, (source, target) in enumerate(
+            (
+                (named_hbm, named_ref),
+                (slot_hbm, slot_ref),
+                (queries_hbm, queries),
+                (lengths_hbm, lengths_ref),
+                (text_lengths_hbm, text_lengths_ref),
+            )
+        )
+    ]
+    for load in first:
+        load.start()
     barrier = pltpu.get_barrier_semaphore()
-
-    def greet(step, carry):
-        pl.semaphore_signal(
-            barrier,
-            inc=1,
-            device_id={"seq": (me + near_place(step)) % devices},
-            device_id_type=MESH,
-        )
-        return carry
-
-    lax.fori_loop(0, close, greet, 0)
-
-    first = pltpu.make_async_copy(queries_hbm, queries, query_sem)
-    first.start()
+    signal(barrier, 1)
+    signal(barrier, 2)
+
     loads = []
     for image in range(held):
         for head in range(local_kv):
@@ -144,9 +167,8 @@
                 )
     loads.append(pltpu.make_async_copy(text_keys_hbm, text_keys, text_sem.at[0]))
     loads.append(pltpu.make_async_copy(text_values_hbm, text_values, text_sem.at[1]))
-    for load in loads:
-        load.start()
-
+    first[0].wait()
+    first[1].wait()
     named = named_ref[...].astype(jnp.float32)
     slot_column = column(slot_ref[...].astype(jnp.float32))
     slot_of = jnp.where(iota((images, rows), 0) == named, slot_column, 0.0)
@@ -162,12 +184,28 @@
     place_in = jnp.where(iota((images * most, rows), 0) == target_row, 1.0, 0.0)
     place_in = place_in.astype(jnp.bfloat16)
     pick[...] = jnp.where(iota((rows, images * most), 1) == target, 1.0, 0.0).astype(jnp.bfloat16)
-    first.wait()
+    first[2].wait()
+    for load in loads:
+        load.start()
     for head in range(heads):
         sent = jnp.dot(place_in, queries[head], preferred_element_type=jnp.float32)
         sent = sent.reshape(devices, slots, size).astype(jnp.bfloat16)
         asked[:, head // group, pl.ds(head % group * slots, slots), :] = sent
 
+    def ask_near(step, carry):
+        ask(near_place(step)).start()
+        return carry
+
+    for stage, (low, high) in enumerate(stages):
+        if stage == 0:
+            pl.semaphore_wait(barrier, 4)
+        else:
+            pl.semaphore_wait(far_sem.at[stage - 1], 2)
+        signal(far_sem.at[stage], high)
+        lax.fori_loop(2 * low, 2 * high, ask_near, 0)
+
+    first[3].wait()
+    first[4].wait()
     row = lax.broadcasted_iota(jnp.int32, (slots, held * tokens), 0)
     token = lax.broadcasted_iota(jnp.int32, (slots, held * tokens), 1)
     valid = jnp.zeros((slots, held * tokens), jnp.bool_)
@@ -177,20 +215,6 @@
         valid = valid | (mine & inside)
     bias[...] = jnp.where(valid, 0.0, NEGATIVE)
 
-    pl.semaphore_wait(barrier, close)
-    for step in range(2):
-        pl.semaphore_signal(
-            far_sem,
-            inc=1,
-            device_id={"seq": (me + near_place(step)) % devices},
-            device_id_type=MESH,
-        )
-
-    def ask_near(step, carry):
-        ask(near_place(step)).start()
-        return carry
-
-    lax.fori_loop(0, close, ask_near, 0)
     for load in loads:
         load.wait()
 
@@ -228,7 +252,7 @@
         return carry
 
     lax.fori_loop(0, rows // CHUNK, read_text, 0)
-    pl.semaphore_wait(far_sem, 2)
+    pl.semaphore_wait(far_sem.at[len(stages) - 1], 2)
 
     def ask_far(step, carry):
         ask(far_place(step)).start()
@@ -285,16 +309,20 @@
         return carry
 
     def send_near(step, carry):
-        send_back(near_place(step))
+        send_back(both(reach - step // 2, step))
+        return carry
+
+    def left(step, carry):
+        ask(step).wait_send()
         return carry
 
     lax.fori_loop(0, close, serve_near, 0)
     lax.fori_loop(0, others - close, serve_far, 0)
     send_back(far_place(others - close - 1))
     lax.fori_loop(0, close, send_near, 0)
+    lax.fori_loop(1, devices, left, 0)
 
     def finish(step, carry):
-        ask(step).wait_send()
         for copy in reply(step):
             copy.wait()
         return carry
@@ -355,14 +383,18 @@
     scale = 1.0 / math.sqrt(size)
     message = (devices, local_kv, heads // local_kv * slots, size)
     vmem = pl.BlockSpec(memory_space=pltpu.VMEM)
-    hbm = pl.BlockSpec(memory_space=pl.ANY)
+    hbm = pl.BlockSpec(memory_space=pltpu.HBM)
     links = pltpu.SemaphoreType.DMA((devices,))
     out = pl.pallas_call(
         functools.partial(kernel, devices, most, scale),
         out_shape=jax.ShapeDtypeStruct((heads, rows, size), jnp.bfloat16),
-        in_specs=[pl.BlockSpec(memory_space=pltpu.SMEM), vmem, vmem, vmem, hbm, hbm, hbm, hbm, hbm],
+        in_specs=[hbm] * 9,
         out_specs=vmem,
         scratch_shapes=[
+            pltpu.SMEM((held,), jnp.int32),
+            pltpu.VMEM((1, rows), jnp.int32),
+            pltpu.VMEM((1, images), jnp.int32),
+            pltpu.VMEM((1, rows), jnp.int32),
             pltpu.VMEM((heads, rows, size), jnp.bfloat16),
             pltpu.VMEM((local_kv, held * tokens, size), jnp.bfloat16),
             pltpu.VMEM((local_kv, held * tokens, size), jnp.bfloat16),
@@ -378,8 +410,8 @@
             pltpu.VMEM((devices, 1, 128), jnp.float32),
             pltpu.VMEM((heads, rows, size), jnp.float32),
             pltpu.VMEM((rows, 128), jnp.float32),
-            pltpu.SemaphoreType.REGULAR,
-            pltpu.SemaphoreType.DMA,
+            pltpu.SemaphoreType.REGULAR((8,)),
+            pltpu.SemaphoreType.DMA((5,)),
             pltpu.SemaphoreType.DMA((2, held, local_kv)),
             pltpu.SemaphoreType.DMA((2,)),
             links,
@@ -390,18 +422,23 @@
             links,
         ],
         compiler_params=pltpu.CompilerParams(
-            collective_id=0, has_side_effects=True, vmem_limit_bytes=62 * 1024 * 1024
+            collective_id=0, has_side_effects=True, vmem_limit_bytes=32 * 1024 * 1024
         ),
     )(
-        image_lengths,
-        request_image.reshape(1, rows),
-        image_slot.reshape(1, images),
-        text_lengths.reshape(1, rows),
-        queries.transpose(1, 0, 2),
-        image_keys,
-        image_values,
-        text_keys,
-        text_values,
+        *(
+            pltpu.with_memory_space_constraint(array, pltpu.HBM)
+            for array in (
+                image_lengths,
+                request_image.reshape(1, rows),
+                image_slot.reshape(1, images),
+                text_lengths.reshape(1, rows),
+                queries.transpose(1, 0, 2),
+                image_keys,
+                image_values,
+                text_keys,
+                text_values,
+            )
+        )
     )
     return out.transpose(1, 0, 2)
 

time: 195 us -> 189 us (0.969)
  Pallas kernels: 193 us -> 188 us
    pallas_call x1, Pallas kernels: 193 us -> 188 us  [on_device(): pl.pallas_call(functools.partial(kernel, devices, most, scale), out_shape...]
where the time goes in v4:
time: 189 us
  Pallas kernels  188 us (99%)
    pallas_call x1, Pallas kernels, on_device(): pl.pallas_call(functools.partial(kernel, devices, most, scale), out_shape...  188 us

profile of v4, /device:TPU:37, one launch (start us, length us, event | category | flops | bytes accessed | tf_op | source)
XLA Modules:
  0.0 189.0 jit_solution(9162289326440664986)
XLA Ops:
  0.0 188.2 %shard_map.91 = bf16[14,128,128]{2,1,0:T(8,128)(2,1)S(1)} custom-call(s32[2]{0:T(128)} %lengths_hbm.1, s32[1,128]{1,0:T(1,128)} %bitcast.7, s32[1,64]{1,0:T(1,128)} %bitcast.8, s32[1,128]{1,0:T(1,128)} %bitcast.9, bf16[14,128,128]{2,1,0:T(8,128)(2,1)} %bitcast.6, bf16[2,2,1280,128]{3,2,1,0:T(8,128)(2,1)} %image_keys_hbm.1, ...), custom_call_target="tpu_custom_call" | custom-call | tf_op jit(solution)/shard_map/pallas_call | solution.py:388
  188.2 0.8 copy.11

commit v5 on v4

--- a/solution.py
+++ b/solution.py
@@ -55,6 +55,7 @@
     back,
     back_lse,
     text_out,
+    shares,
     text_lse,
     far_sem,
     first_sem,
@@ -108,24 +109,23 @@
         )
 
     def reply(at):
-        target = {"seq": (me + devices - at) % devices}
-        return (
-            pltpu.make_async_remote_copy(
-                src_ref=answer.at[at],
-                dst_ref=back.at[at],
-                send_sem=out_send.at[at],
-                recv_sem=out_recv.at[at],
-                device_id=target,
-                device_id_type=MESH,
-            ),
-            pltpu.make_async_remote_copy(
-                src_ref=answer_lse.at[at],
-                dst_ref=back_lse.at[at],
-                send_sem=lse_send.at[at],
-                recv_sem=lse_recv.at[at],
-                device_id=target,
-                device_id_type=MESH,
-            ),
+        return pltpu.make_async_remote_copy(
+            src_ref=answer.at[at],
+            dst_ref=back.at[at],
+            send_sem=out_send.at[at],
+            recv_sem=out_recv.at[at],
+            device_id={"seq": (me + devices - at) % devices},
+            device_id_type=MESH,
+        )
+
+    def reply_lse(at):
+        return pltpu.make_async_remote_copy(
+            src_ref=answer_lse.at[at],
+            dst_ref=back_lse.at[at],
+            send_sem=lse_send.at[at],
+            recv_sem=lse_recv.at[at],
+            device_id={"seq": (me + devices - at) % devices},
+            device_id_type=MESH,
         )
 
     def signal(sem, hops):
@@ -292,42 +292,44 @@
         ask(at).wait_recv()
         attend(incoming, at, answer, answer_lse)
 
-    def send_back(at):
-        for copy in reply(at):
-            copy.start()
-
     def serve_near(step, carry):
+        @pl.when(step > 0)
+        def _():
+            reply_lse(near_place(step - 1)).start()
+
         serve(near_place(step))
         return carry
 
     def serve_far(step, carry):
         @pl.when(step > 0)
         def _():
-            send_back(far_place(step - 1))
+            reply(far_place(step - 1)).start()
+            reply_lse(far_place(step - 1)).start()
 
         serve(far_place(step))
         return carry
 
     def send_near(step, carry):
-        send_back(both(reach - step // 2, step))
-        return carry
-
-    def left(step, carry):
+        reply(both(reach - step // 2, step)).start()
+        return carry
+
+    lax.fori_loop(0, close, serve_near, 0)
+    reply_lse(near_place(close - 1)).start()
+    lax.fori_loop(0, others - close, serve_far, 0)
+    reply(far_place(others - close - 1)).start()
+    reply_lse(far_place(others - close - 1)).start()
+    lax.fori_loop(0, close, send_near, 0)
+
+    def settle(step, carry):
         ask(step).wait_send()
-        return carry
-
-    lax.fori_loop(0, close, serve_near, 0)
-    lax.fori_loop(0, others - close, serve_far, 0)
-    send_back(far_place(others - close - 1))
-    lax.fori_loop(0, close, send_near, 0)
-    lax.fori_loop(1, devices, left, 0)
+        reply_lse(step).wait()
+        return carry
 
     def finish(step, carry):
-        for copy in reply(step):
-            copy.wait()
-        return carry
-
-    lax.fori_loop(1, devices, finish, 0)
+        reply(step).wait()
+        return carry
+
+    lax.fori_loop(1, devices, settle, 0)
 
     target = column(target_row)
     from_at = iota((rows, devices), 1) * slots
@@ -354,13 +356,20 @@
     image_weight = jnp.exp(image_lse - top)
     text_weight = jnp.exp(text_lse[...] - top)
     whole = image_weight + text_weight
+    image_share = image_weight / whole
+    text_share = text_weight / whole
+    for head in range(heads):
+        text_out[head] = text_out[head] * text_share[:, head : head + 1]
+        shares[head] = jnp.broadcast_to(image_share[:, head : head + 1], (rows, size))
+
+    lax.fori_loop(reach + 1, devices - reach, finish, 0)
+    lax.fori_loop(1, reach + 1, finish, 0)
+    lax.fori_loop(devices - reach, devices, finish, 0)
     for head in range(heads):
         came = back[:, head // group, pl.ds(head % group * slots, slots), :]
-        came = came.astype(jnp.float32).reshape(devices * slots, size).astype(jnp.bfloat16)
+        came = came.reshape(devices * slots, size)
         image_out = jnp.dot(pick[...], came, preferred_element_type=jnp.float32)
-        merged = image_weight[:, head : head + 1] * image_out
-        merged = merged + text_weight[:, head : head + 1] * text_out[head]
-        out_ref[head] = (merged / whole[:, head : head + 1]).astype(jnp.bfloat16)
+        out_ref[head] = (shares[head] * image_out + text_out[head]).astype(jnp.bfloat16)
 
 
 def on_device(
@@ -409,6 +418,7 @@
             pltpu.VMEM(message, jnp.bfloat16),
             pltpu.VMEM((devices, 1, 128), jnp.float32),
             pltpu.VMEM((heads, rows, size), jnp.float32),
+            pltpu.VMEM((heads, rows, size), jnp.float32),
             pltpu.VMEM((rows, 128), jnp.float32),
             pltpu.SemaphoreType.REGULAR((8,)),
             pltpu.SemaphoreType.DMA((5,)),

time: 189 us -> 188 us (level)
  no operation moved by 1% of the time
where the time goes in v5:
time: 188 us
  Pallas kernels  187 us (99%)
    pallas_call x1, Pallas kernels, on_device(): pl.pallas_call(functools.partial(kernel, devices, most, scale), out_shape...  187 us

profile of v5, /device:TPU:37, one launch (start us, length us, event | category | flops | bytes accessed | tf_op | source)
XLA Modules:
  0.0 188.0 jit_solution(4427556263824824150)
XLA Ops:
  0.0 187.2 %shard_map.91 = bf16[14,128,128]{2,1,0:T(8,128)(2,1)S(1)} custom-call(s32[2]{0:T(128)} %lengths_hbm.1, s32[1,128]{1,0:T(1,128)} %bitcast.7, s32[1,64]{1,0:T(1,128)} %bitcast.8, s32[1,128]{1,0:T(1,128)} %bitcast.9, bf16[14,128,128]{2,1,0:T(8,128)(2,1)} %bitcast.6, bf16[2,2,1280,128]{3,2,1,0:T(8,128)(2,1)} %image_keys_hbm.1, ...), custom_call_target="tpu_custom_call" | custom-call | tf_op jit(solution)/shard_map/pallas_call | solution.py:397
  187.2 0.8 copy.11

commit v6 on v5

--- a/solution.py
+++ b/solution.py
@@ -180,30 +180,37 @@
     earlier = iota((rows, rows), 0) < iota((rows, rows), 1)
     rank = jnp.sum(jnp.where(same & earlier, 1.0, 0.0), axis=0, keepdims=True)
     target_row = near * most + rank
-    target = column(target_row)
-    place_in = jnp.where(iota((images * most, rows), 0) == target_row, 1.0, 0.0)
-    place_in = place_in.astype(jnp.bfloat16)
-    pick[...] = jnp.where(iota((rows, images * most), 1) == target, 1.0, 0.0).astype(jnp.bfloat16)
+    pl.semaphore_wait(barrier, 4)
+    signal(far_sem.at[0], stages[0][1])
     first[2].wait()
     for load in loads:
         load.start()
-    for head in range(heads):
-        sent = jnp.dot(place_in, queries[head], preferred_element_type=jnp.float32)
-        sent = sent.reshape(devices, slots, size).astype(jnp.bfloat16)
-        asked[:, head // group, pl.ds(head % group * slots, slots), :] = sent
+
+    def dispatch(ranges):
+        for low, high in ranges:
+            number = (high - low) * slots
+            place_in = iota((number, rows), 0) + low * slots == target_row
+            place_in = jnp.where(place_in, 1.0, 0.0).astype(jnp.bfloat16)
+            for head in range(heads):
+                sent = jnp.dot(place_in, queries[head], preferred_element_type=jnp.float32)
+                sent = sent.reshape(high - low, slots, size).astype(jnp.bfloat16)
+                asked[low:high, head // group, pl.ds(head % group * slots, slots), :] = sent
+
+    dispatch(((0, reach + 1), (devices - reach, devices)))
 
     def ask_near(step, carry):
         ask(near_place(step)).start()
         return carry
 
     for stage, (low, high) in enumerate(stages):
-        if stage == 0:
-            pl.semaphore_wait(barrier, 4)
-        else:
+        if stage > 0:
             pl.semaphore_wait(far_sem.at[stage - 1], 2)
-        signal(far_sem.at[stage], high)
+            signal(far_sem.at[stage], high)
         lax.fori_loop(2 * low, 2 * high, ask_near, 0)
 
+    dispatch(((reach + 1, devices - reach),))
+    target = column(target_row)
+    pick[...] = jnp.where(iota((rows, images * most), 1) == target, 1.0, 0.0).astype(jnp.bfloat16)
     first[3].wait()
     first[4].wait()
     row = lax.broadcasted_iota(jnp.int32, (slots, held * tokens), 0)

time: 188 us -> 188 us (level)
  no operation moved by 1% of the time
where the time goes in v6:
time: 188 us
  Pallas kernels  187 us (99%)
    pallas_call x1, Pallas kernels, on_device(): pl.pallas_call(functools.partial(kernel, devices, most, scale), out_shape...  187 us

profile of v6, /device:TPU:37, one launch (start us, length us, event | category | flops | bytes accessed | tf_op | source)
XLA Modules:
  0.0 187.7 jit_solution(11327751643486210939)
XLA Ops:
  0.0 186.9 %shard_map.91 = bf16[14,128,128]{2,1,0:T(8,128)(2,1)S(1)} custom-call(s32[2]{0:T(128)} %lengths_hbm.1, s32[1,128]{1,0:T(1,128)} %bitcast.7, s32[1,64]{1,0:T(1,128)} %bitcast.8, s32[1,128]{1,0:T(1,128)} %bitcast.9, bf16[14,128,128]{2,1,0:T(8,128)(2,1)} %bitcast.6, bf16[2,2,1280,128]{3,2,1,0:T(8,128)(2,1)} %image_keys_hbm.1, ...), custom_call_target="tpu_custom_call" | custom-call | tf_op jit(solution)/shard_map/pallas_call | solution.py:404
  186.9 0.8 copy.11

commit v7 on v6

--- a/solution.py
+++ b/solution.py
@@ -83,6 +83,10 @@
     while stages[-1][1] < reach:
         stages.append((stages[-1][1], 2 * stages[-1][1]))
 
+    def ring(at):
+        spot_at = me + at
+        return spot_at - (spot_at >= devices) * devices
+
     def both(hops, step):
         return hops + (step % 2) * (devices - 2 * hops)
 
@@ -104,7 +108,7 @@
             dst_ref=incoming.at[at],
             send_sem=ask_send.at[at],
             recv_sem=ask_recv.at[at],
-            device_id={"seq": (me + at) % devices},
+            device_id={"seq": ring(at)},
             device_id_type=MESH,
         )
 
@@ -114,7 +118,7 @@
             dst_ref=back.at[at],
             send_sem=out_send.at[at],
             recv_sem=out_recv.at[at],
-            device_id={"seq": (me + devices - at) % devices},
+            device_id={"seq": ring(devices - at)},
             device_id_type=MESH,
         )
 
@@ -124,14 +128,14 @@
             dst_ref=back_lse.at[at],
             send_sem=lse_send.at[at],
             recv_sem=lse_recv.at[at],
-            device_id={"seq": (me + devices - at) % devices},
+            device_id={"seq": ring(devices - at)},
             device_id_type=MESH,
         )
 
     def signal(sem, hops):
         for at in (hops, devices - hops):
             pl.semaphore_signal(
-                sem, inc=1, device_id={"seq": (me + at) % devices}, device_id_type=MESH
+                sem, inc=1, device_id={"seq": ring(at)}, device_id_type=MESH
             )
 
     first = [
@@ -187,14 +191,21 @@
         load.start()
 
     def dispatch(ranges):
+        number = sum(high - low for low, high in ranges) * slots
+        line = iota((number, rows), 0)
+        at, shift = line, 0
         for low, high in ranges:
-            number = (high - low) * slots
-            place_in = iota((number, rows), 0) + low * slots == target_row
-            place_in = jnp.where(place_in, 1.0, 0.0).astype(jnp.bfloat16)
-            for head in range(heads):
-                sent = jnp.dot(place_in, queries[head], preferred_element_type=jnp.float32)
-                sent = sent.reshape(high - low, slots, size).astype(jnp.bfloat16)
-                asked[low:high, head // group, pl.ds(head % group * slots, slots), :] = sent
+            at = jnp.where(line >= shift, line + (low * slots - shift), at)
+            shift += (high - low) * slots
+        place_in = jnp.where(at == target_row, 1.0, 0.0).astype(jnp.bfloat16)
+        for head in range(heads):
+            sent = jnp.dot(place_in, queries[head], preferred_element_type=jnp.float32)
+            sent = sent.reshape(number // slots, slots, size).astype(jnp.bfloat16)
+            start = 0
+            for low, high in ranges:
+                piece = sent[start : start + high - low]
+                asked[low:high, head // group, pl.ds(head % group * slots, slots), :] = piece
+                start += high - low
 
     dispatch(((0, reach + 1), (devices - reach, devices)))
 

time: 188 us -> 188 us (level)
  no operation moved by 1% of the time
where the time goes in v7:
time: 188 us
  Pallas kernels  187 us (99%)
    pallas_call x1, Pallas kernels, on_device(): pl.pallas_call(functools.partial(kernel, devices, most, scale), out_shape...  187 us

profile of v7, /device:TPU:37, one launch (start us, length us, event | category | flops | bytes accessed | tf_op | source)
XLA Modules:
  0.0 187.7 jit_solution(3540185943896188954)
XLA Ops:
  0.0 187.0 %shard_map.91 = bf16[14,128,128]{2,1,0:T(8,128)(2,1)S(1)} custom-call(s32[2]{0:T(128)} %lengths_hbm.1, s32[1,128]{1,0:T(1,128)} %bitcast.7, s32[1,64]{1,0:T(1,128)} %bitcast.8, s32[1,128]{1,0:T(1,128)} %bitcast.9, bf16[14,128,128]{2,1,0:T(8,128)(2,1)} %bitcast.6, bf16[2,2,1280,128]{3,2,1,0:T(8,128)(2,1)} %image_keys_hbm.1, ...), custom_call_target="tpu_custom_call" | custom-call | tf_op jit(solution)/shard_map/pallas_call | solution.py:415
  187.0 0.8 copy.11
